TPU v7x, 512 devices: a whole 4x4x16 slice. The times are simulated.
512 devices in a mesh: row: 32 (over x_lo, z), col: 16 (over y, x_hi, core).
Axes of the slice: x: 4 (x_hi: 2, x_lo: 2; x = x_hi * 2 + x_lo), y: 4, z: 16, core: 2. Of those that a mesh axis runs over, the one named last changes fastest.
Arguments:
- gradient: bfloat16 [8192, 28672], P('row', 'col'), may hold values from -6 to 6
- projector: bfloat16 [8192, 1024], P('row'), may hold values from -0.375 to 0.375
- first_moment: float32 [1024, 28672], P('row', 'col'), may hold values from -6 to 6
- second_moment: float32 [1024, 28672], P('row', 'col'), may hold values from 5e-05 to 0.12, as said below
Outputs:
- update: bfloat16 [8192, 28672], P('row', 'col')
- first_new: float32 [1024, 28672], P('row', 'col')
- second_new: float32 [1024, 28672], P('row', 'col')
Inputs may be any that keep to these rules, and one draw needn't show every extreme that they name: `second_moment`: entries are positive.
All inputs are finite; a program needn't handle non-finite values.
Results may differ from a plain program's by a relative error of at most 0.038.
Values may be sent and summed in bfloat16 or wider, within the bound.
No kernel may reach another device: no remote copies, remote signals or barrier semaphores. Data moves between devices by JAX's collectives and lax.ppermute only.
A program may use at most 64 MiB of HBM per device.

v0:
```python
import jax
import jax.numpy as jnp
from jax import lax
from jax.sharding import Mesh
from jax.sharding import PartitionSpec as P

FF = 28672
R = 1024
LANES = 128
ROW = ("x_lo", "z_hi", "z_lo")
COL = ("y", "x_hi", "core")
SQUARE = ("x_lo", "z_lo")
decay_first = 0.9
decay_second = 0.999
bias_first = 1.0 - 0.9**10
bias_second = 1.0 - 0.999**10
epsilon = 1e-08
clip_limit = 0.5


def exchanged(pieces, axes):
    return lax.all_to_all(pieces, axes, split_axis=0, concat_axis=0, tiled=True)


def spread(block, axes):
    return exchanged(jnp.broadcast_to(block, (lax.axis_size(axes), *block.shape)), axes)


def column_blocks(array, parts, width):
    rows, columns = array.shape
    array = jnp.pad(array, ((0, 0), (0, parts * width - columns)))
    return array.reshape(rows, parts, width).swapaxes(0, 1)


def side_by_side(blocks, columns):
    return blocks.swapaxes(0, 1).reshape(blocks.shape[1], -1)[:, :columns]


def summed_everywhere(value):
    value = jnp.full((8, LANES), value, jnp.float32)
    for axes in (SQUARE, "z_hi", COL):
        value = jnp.sum(spread(value, axes), axis=0)
    return value[0, 0]


def local(gradient, projector, first_moment, second_moment):
    block_rows, columns = gradient.shape
    ranks = projector.shape[1]
    rows = first_moment.shape[0]
    square = lax.axis_size(SQUARE)
    z_hi, z_lo = (lax.axis_size("z_hi"), lax.axis_size("z_lo"))
    width = -(-columns // (square * LANES)) * LANES
    half = ranks // 2
    basis = projector.reshape(block_rows, -1, z_hi, z_lo * rows).swapaxes(1, 2)
    basis = basis.reshape(block_rows, ranks)
    own_half = lax.dynamic_slice_in_dim(basis, lax.axis_index("core") * half, half, 1)
    halves = spread(spread(own_half, SQUARE).reshape(square * block_rows, half), "core")
    block = exchanged(column_blocks(gradient, square, width), SQUARE)
    block = block.reshape(square * block_rows, width)
    partial = jnp.concatenate(
        [
            lax.dot_general(
                halves[k], block, (((0,), (0,)), ((), ())), preferred_element_type=jnp.float32
            ).astype(jnp.bfloat16)
            for k in range(2)
        ]
    )
    summed = lax.psum_scatter(
        partial.reshape(z_hi, ranks // z_hi, width), "z_hi", scatter_dimension=0, tiled=True
    )
    lowrank = exchanged(summed.reshape(square, rows, width), SQUARE)
    lowrank = side_by_side(lowrank, columns).astype(jnp.float32)
    first_new = decay_first * first_moment + (1.0 - decay_first) * lowrank
    second_new = decay_second * second_moment + (1.0 - decay_second) * lowrank * lowrank
    direction = first_new / bias_first / (jnp.sqrt(second_new / bias_second) + epsilon)
    step = exchanged(column_blocks(direction.astype(jnp.bfloat16), square, width), SQUARE)
    step = lax.all_gather(step.reshape(square * rows, width), "z_hi", axis=0, tiled=True)
    total = summed_everywhere(jnp.sum(direction * direction))
    root_mean = jnp.sqrt(total / (R * FF) + 1e-06)
    factor = jnp.minimum(1.0, clip_limit / root_mean)
    whole = lax.optimization_barrier(jnp.concatenate([halves[0], halves[1]], axis=1))
    projected = jnp.dot(whole, step, preferred_element_type=jnp.float32)
    updates = (factor * projected).astype(jnp.bfloat16)
    updates = exchanged(updates.reshape(square, block_rows, width), SQUARE)
    return (side_by_side(updates, columns), first_new, second_new)


def solution(mesh):
    torus = Mesh(mesh.devices.reshape(2, 8, 2, 4, 2, 2), (*ROW, *COL))
    in_specs = (P(ROW, COL), P(ROW, None), P(ROW, COL), P(ROW, COL))
    out_specs = (P(ROW, COL), P(ROW, COL), P(ROW, COL))
    return jax.shard_map(local, mesh=torus, in_specs=in_specs, out_specs=out_specs, check_vma=False)
```

profile of v0, /device:TPU:4, one launch (start us, length us, event | category | flops | bytes accessed | tf_op | source)
XLA Modules:
  0.0 203.9 jit_solution(18431546739833409747)
XLA Ops:
  7.2 1.2 copy.37
  8.5 0.0 copy-start.3
  8.5 0.1 copy.39
  8.7 1.0 broadcast_in_dim.12
  9.7 3.8 %all-to-all-start = ((bf16[4,256,512]{2,1,0:T(8,128)(2,1)}), bf16[4,256,512]{2,1,0:T(8,128)(2,1)S(1)}, u32[]{:S(2)}, u32[]{:S(2)}) async-start(bf16[4,256,512]{2,1,0:T(8,128)(2,1)} %broadcast_in_dim.12), calls=%async_computation | async-start | bytes 2097152 | tf_op jit(solution)/shard_map/all_to_all | solution.py:22
  13.5 0.0 copy-done.3
  13.5 0.5 copy.40
  14.1 0.1 pad.8
  14.1 13.1 %all-to-all-done = bf16[4,256,512]{2,1,0:T(8,128)(2,1)S(1)} async-done(((bf16[4,256,512]{2,1,0:T(8,128)(2,1)}), bf16[4,256,512]{2,1,0:T(8,128)(2,1)S(1)}, u32[]{:S(2)}, u32[]{:S(2)}) %all-to-all-start) | async-done | bytes 1048608 | tf_op jit(solution)/shard_map/all_to_all | solution.py:22
  27.3 15.9 %all_to_all.45 = bf16[4,256,512]{1,2,0:T(8,128)(2,1)S(1)} all-to-all(bf16[4,256,512]{1,2,0:T(8,128)(2,1)S(1)} %bitcast.33), channel_id=1, replica_groups=mesh['x_lo'=2,'z_hi'=8,'z_lo'=2,'y'=4,'x_hi'=2,'core'=2] {'x_lo','z_lo'}, dimensions={0} | all-to-all | bytes 2097152 | tf_op jit(solution)/shard_map/all_to_all | solution.py:22
  43.2 1.5 broadcast_in_dim.13
  44.7 3.8 %all-to-all-start.1 = ((bf16[2,1024,512]{2,1,0:T(8,128)(2,1)}), bf16[2,1024,512]{2,1,0:T(8,128)(2,1)S(1)}, u32[]{:S(2)}, u32[]{:S(2)}) async-start(bf16[2,1024,512]{2,1,0:T(8,128)(2,1)} %broadcast_in_dim.13), calls=%async_computation.1 | async-start | bytes 4194304 | tf_op jit(solution)/shard_map/all_to_all | solution.py:22
  48.5 0.0 reduce-scatter.2.cloned.1.call-start
  48.5 1.3 copy.41
  49.9 1.5 all-to-all-done.1
  51.3 2.0 convolution_convert_fusion.1
  53.3 0.0 copy-done
  53.3 0.7 convolution_convert_fusion
  54.1 0.0 copy-start.4
  54.1 0.0 copy-start.5
  54.1 1.0 pad_maximum_fusion.1
  55.1 0.0 reduce-scatter.2.cloned.1.call-update
  55.1 0.0 all-gather.2.cloned.1.call-start
  55.2 57.3 %reduce-scatter.2.cloned.1.call-done = bf16[1,128,512]{2,1,0:T(8,128)(2,1)} async-done(((bf16[8,128,512]{2,1,0:T(8,128)(2,1)}), bf16[1,128,512]{2,1,0:T(8,128)(2,1)}) %reduce-scatter.2.cloned.1.call-update) | async-done | bytes 131088 | tf_op jit(solution)/shard_map/reduce_scatter | solution.py:68
  112.5 8.3 %all_to_all.46 = bf16[4,32,512]{2,1,0:T(8,128)(2,1)S(1)} all-to-all(bf16[4,32,512]{2,1,0:T(8,128)(2,1)} %bitcast.45), channel_id=1, replica_groups=mesh['x_lo'=2,'z_hi'=8,'z_lo'=2,'y'=4,'x_hi'=2,'core'=2] {'x_lo','z_lo'}, dimensions={0} | all-to-all | bytes 262144 | tf_op jit(solution)/shard_map/all_to_all | solution.py:22
  120.8 0.0 copy-done.4
  120.8 0.0 copy-done.5
  120.8 0.8 multiply_reduce_fusion
  121.6 0.1 fusion.2
  121.7 0.1 reshape.57
  121.8 8.1 %all_to_all.47 = bf16[4,32,512]{2,1,0:T(8,128)(2,1)} all-to-all(bf16[4,32,512]{2,1,0:T(8,128)(2,1)S(1)} %copy.43), channel_id=1, replica_groups=mesh['x_lo'=2,'z_hi'=8,'z_lo'=2,'y'=4,'x_hi'=2,'core'=2] {'x_lo','z_lo'}, dimensions={0} | all-to-all | bytes 262144 | tf_op jit(solution)/shard_map/all_to_all | solution.py:22
  129.9 0.0 all-gather.2.cloned.1.call-update
  129.9 0.6 broadcast_in_dim_broadcast_in_dim.3
  130.6 7.1 %all_to_all.48 = f32[4,8,128]{2,1,0:T(8,128)S(1)} all-to-all(f32[4,8,128]{2,1,0:T(8,128)S(1)} %broadcast_in_dim_broadcast_in_dim.3), channel_id=1, replica_groups=mesh['x_lo'=2,'z_hi'=8,'z_lo'=2,'y'=4,'x_hi'=2,'core'=2] {'x_lo','z_lo'}, dimensions={0} | all-to-all | bytes 32768 | tf_op jit(solution)/shard_map/all_to_all | solution.py:22
  137.6 0.6 broadcast_in_dim.14
  138.3 7.5 %all-to-all-start.5 = ((f32[8,8,128]{2,1,0:T(8,128)}), f32[8,8,128]{2,1,0:T(8,128)S(1)}, u32[]{:S(2)}, u32[]{:S(2)}) async-start(f32[8,8,128]{2,1,0:T(8,128)} %broadcast_in_dim.14), calls=%async_computation.6 | async-start | bytes 65536 | tf_op jit(solution)/shard_map/all_to_all | solution.py:22
  145.8 1.2 slice_bitcast_fusion.1
  147.0 11.8 %all-to-all-done.5 = f32[8,8,128]{2,1,0:T(8,128)S(1)} async-done(((f32[8,8,128]{2,1,0:T(8,128)}), f32[8,8,128]{2,1,0:T(8,128)S(1)}, u32[]{:S(2)}, u32[]{:S(2)}) %all-to-all-start.5) | async-done | bytes 32800 | tf_op jit(solution)/shard_map/all_to_all | solution.py:22
  158.8 0.6 broadcast_in_dim.15
  159.4 7.3 %all-to-all-start.6 = ((f32[16,8,128]{2,1,0:T(8,128)}), f32[16,8,128]{2,1,0:T(8,128)S(1)}, u32[]{:S(2)}, u32[]{:S(2)}) async-start(f32[16,8,128]{2,1,0:T(8,128)} %broadcast_in_dim.15), calls=%async_computation.7 | async-start | bytes 131072 | tf_op jit(solution)/shard_map/all_to_all | solution.py:22
  166.7 1.5 pad_maximum_fusion
  168.2 3.4 %all-to-all-done.6 = f32[16,8,128]{2,1,0:T(8,128)S(1)} async-done(((f32[16,8,128]{2,1,0:T(8,128)}), f32[16,8,128]{2,1,0:T(8,128)S(1)}, u32[]{:S(2)}, u32[]{:S(2)}) %all-to-all-start.6) | async-done | bytes 65568 | tf_op jit(solution)/shard_map/all_to_all | solution.py:22
  171.6 0.5 slice.20
  172.8 6.0 %all-gather.2.cloned.1.call-done = bf16[1024,512]{1,0:T(8,128)(2,1)} async-done(((bf16[128,512]{1,0:T(8,128)(2,1)}), bf16[1024,512]{1,0:T(8,128)(2,1)}) %all-gather.2.cloned.1.call-update) | async-done | bytes 1048592 | tf_op jit(solution)/shard_map/all_gather | solution.py:77
  178.8 2.5 %multiply_convert_fusion = bf16[1024,512]{1,0:T(8,128)(2,1)S(1)} fusion(bf16[1024,1024]{1,0:T(8,128)(2,1)S(1)} %pad_maximum_fusion, bf16[1024,512]{1,0:T(8,128)(2,1)} %all-gather.2.cloned.1.call-done, f32[]{:T(128)} %bitcast.12), kind=kOutput, calls=%fused_computation.1 | convolution fusion | flops 1074790400 | bytes 4194308 | tf_op jit(solution)/shard_map/dot_general | solution.py:82
  181.3 14.6 %all_to_all.49 = bf16[4,256,512]{2,1,0:T(8,128)(2,1)S(1)} all-to-all(bf16[4,256,512]{2,1,0:T(8,128)(2,1)S(1)} %bitcast.40), channel_id=1, replica_groups=mesh['x_lo'=2,'z_hi'=8,'z_lo'=2,'y'=4,'x_hi'=2,'core'=2] {'x_lo','z_lo'}, dimensions={0} | all-to-all | bytes 2097152 | tf_op jit(solution)/shard_map/all_to_all | solution.py:22
  195.9 0.1 copy.46
  196.0 1.0 slice.25
  (13 shorter events, 0.2 us)
Async XLA Ops:
  8.5 5.0 %copy-start.3 = (bf16[256,1792]{1,0:T(8,128)(2,1)S(1)}, bf16[256,1792]{1,0:T(8,128)(2,1)}, u32[]{:S(2)}) copy-start(bf16[256,1792]{1,0:T(8,128)(2,1)} %param.4) | copy-start | bytes 2752516
  9.7 17.6 %all-to-all-start = ((bf16[4,256,512]{2,1,0:T(8,128)(2,1)}), bf16[4,256,512]{2,1,0:T(8,128)(2,1)S(1)}, u32[]{:S(2)}, u32[]{:S(2)}) async-start(bf16[4,256,512]{2,1,0:T(8,128)(2,1)} %broadcast_in_dim.12), calls=%async_computation | async-start | bytes 2097152 | tf_op jit(solution)/shard_map/all_to_all | solution.py:22
  44.7 6.6 %all-to-all-start.1 = ((bf16[2,1024,512]{2,1,0:T(8,128)(2,1)}), bf16[2,1024,512]{2,1,0:T(8,128)(2,1)S(1)}, u32[]{:S(2)}, u32[]{:S(2)}) async-start(bf16[2,1024,512]{2,1,0:T(8,128)(2,1)} %broadcast_in_dim.13), calls=%async_computation.1 | async-start | bytes 4194304 | tf_op jit(solution)/shard_map/all_to_all | solution.py:22
  48.5 64.0 %reduce-scatter.2.cloned.1.call-start = ((), (), s32[]{:S(2)}) async-start(), calls=%async_computation.10 | async-start | bytes 1179648 | tf_op jit(solution)/shard_map/reduce_scatter | solution.py:68
  49.9 3.4 %copy-start = (bf16[4,256,512]{2,1,0:T(8,128)(2,1)S(1)}, bf16[4,256,512]{2,1,0:T(8,128)(2,1)}, u32[]{:S(2)}) copy-start(bf16[4,256,512]{2,1,0:T(8,128)(2,1)} %copy.41) | copy-start | bytes 3145732
  54.1 66.7 %copy-start.4 = (f32[32,1792]{1,0:T(8,128)S(1)}, f32[32,1792]{1,0:T(8,128)}, u32[]{:S(2)}) copy-start(f32[32,1792]{1,0:T(8,128)} %param.6) | copy-start | bytes 688132
  54.1 66.7 %copy-start.5 = (f32[32,1792]{1,0:T(8,128)S(1)}, f32[32,1792]{1,0:T(8,128)}, u32[]{:S(2)}) copy-start(f32[32,1792]{1,0:T(8,128)} %param.7) | copy-start | bytes 688132
  55.1 123.6 %all-gather.2.cloned.1.call-start = ((), (), s32[]{:S(2)}) async-start(), calls=%async_computation.11 | async-start | bytes 1179648 | tf_op jit(solution)/shard_map/all_gather | solution.py:77
  121.6 16.7 %copy-start.2 = (f32[32,1792]{1,0:T(8,128)}, f32[32,1792]{1,0:T(8,128)S(1)}, u32[]{:S(2)}) copy-start(f32[32,1792]{1,0:T(8,128)S(1)} %get-tuple-element.5) | copy-start | bytes 688132
  121.6 25.4 %copy-start.1 = (f32[32,1792]{1,0:T(8,128)}, f32[32,1792]{1,0:T(8,128)S(1)}, u32[]{:S(2)}) copy-start(f32[32,1792]{1,0:T(8,128)S(1)} %get-tuple-element.4) | copy-start | bytes 688132
  138.3 20.5 %all-to-all-start.5 = ((f32[8,8,128]{2,1,0:T(8,128)}), f32[8,8,128]{2,1,0:T(8,128)S(1)}, u32[]{:S(2)}, u32[]{:S(2)}) async-start(f32[8,8,128]{2,1,0:T(8,128)} %broadcast_in_dim.14), calls=%async_computation.6 | async-start | bytes 65536 | tf_op jit(solution)/shard_map/all_to_all | solution.py:22
  159.4 12.1 %all-to-all-start.6 = ((f32[16,8,128]{2,1,0:T(8,128)}), f32[16,8,128]{2,1,0:T(8,128)S(1)}, u32[]{:S(2)}, u32[]{:S(2)}) async-start(f32[16,8,128]{2,1,0:T(8,128)} %broadcast_in_dim.15), calls=%async_computation.7 | async-start | bytes 131072 | tf_op jit(solution)/shard_map/all_to_all | solution.py:22
Sparse Core Ops, SparseCore 0:
  55.3 57.1 reduce-scatter.1
  130.0 48.7 all-gather.1
where the time goes:
time: 205 us; the launch traced here: 204 us
  waiting for transfers between devices  93.1 us (45%)
  blocking collectives  54 us (26%)
  starting transfers between devices  22.5 us (11%)
  between operations  14.9 us (7%)
  local copies, waits for them, and re-layouts  10.8 us (5%)
  matrix products  5.16 us (3%)
  other arithmetic  3.44 us (2%)
    reduce_scatter x1, waiting for transfers between devices, local(): lax.psum_scatter(partial.reshape(z_hi, ranks // z_hi, width), 'z_hi', sca...  57.3 us
    all_to_all x5, blocking collectives, exchanged(): return lax.all_to_all(pieces, axes, split_axis=0, concat_axis=0, tiled=True)  54 us
    all_to_all x4, waiting for transfers between devices, exchanged(): return lax.all_to_all(pieces, axes, split_axis=0, concat_axis=0, tiled=True)  29.8 us
    all_to_all x4, starting transfers between devices, exchanged(): return lax.all_to_all(pieces, axes, split_axis=0, concat_axis=0, tiled=True)  22.4 us
    all_gather x1, waiting for transfers between devices, local(): lax.all_gather(step.reshape(square * rows, width), 'z_hi', axis=0, tiled=...  6 us
  transfers between devices with their start and end apart: 6, of which 6 were waited for; matrix products, arithmetic and copies ran while one was open for 3% of the time, Pallas kernels for 0%

commit v1 on v0

--- a/solution.py
+++ b/solution.py
@@ -74,7 +74,10 @@
     second_new = decay_second * second_moment + (1.0 - decay_second) * lowrank * lowrank
     direction = first_new / bias_first / (jnp.sqrt(second_new / bias_second) + epsilon)
     step = exchanged(column_blocks(direction.astype(jnp.bfloat16), square, width), SQUARE)
-    step = lax.all_gather(step.reshape(square * rows, width), "z_hi", axis=0, tiled=True)
+    vec = step.reshape(square * rows, width)
+    high = jnp.stack(lax.axis_size("z_hi") * [vec])
+    later = lax.all_to_all(high, "z_hi", split_axis=0, concat_axis=0)
+    step = jnp.concatenate(later, axis=0)
     total = summed_everywhere(jnp.sum(direction * direction))
     root_mean = jnp.sqrt(total / (R * FF) + 1e-06)
     factor = jnp.minimum(1.0, clip_limit / root_mean)

time: 205 us -> 256 us (1.25)
  the two profiles are of different devices: /device:TPU:4 before, /device:TPU:64 now
where the time goes in v1:
time: 256 us; the launch traced here: 255 us
  waiting for transfers between devices  130 us (51%)
  blocking collectives  72.8 us (28%)
  starting transfers between devices  20.6 us (8%)
  between operations  14.9 us (6%)
  local copies, waits for them, and re-layouts  10.2 us (4%)
  matrix products  3.92 us (2%)
    all_to_all x6, blocking collectives, exchanged(): return lax.all_to_all(pieces, axes, split_axis=0, concat_axis=0, tiled=True)  72.8 us
    reduce_scatter x1, waiting for transfers between devices, local(): lax.psum_scatter(partial.reshape(z_hi, ranks // z_hi, width), 'z_hi', sca...  57.1 us
    all_to_all x1, waiting for transfers between devices, local(): later = lax.all_to_all(high, 'z_hi', split_axis=0, concat_axis=0)  51.5 us
    all_to_all x3, waiting for transfers between devices, exchanged(): return lax.all_to_all(pieces, axes, split_axis=0, concat_axis=0, tiled=True)  21.9 us
    all_to_all x3, starting transfers between devices, exchanged(): return lax.all_to_all(pieces, axes, split_axis=0, concat_axis=0, tiled=True)  14.5 us
    all_to_all x1, starting transfers between devices, local(): later = lax.all_to_all(high, 'z_hi', split_axis=0, concat_axis=0)  6.08 us
  transfers between devices with their start and end apart: 5, of which 5 were waited for; matrix products, arithmetic and copies ran while one was open for 1% of the time, Pallas kernels for 0%

profile of v1, /device:TPU:64, one launch (start us, length us, event | category | flops | bytes accessed | tf_op | source)
XLA Modules:
  0.0 255.1 jit_solution(2782611862569417278)
XLA Ops:
  7.2 1.2 copy.37
  8.5 0.0 copy-start.3
  8.5 0.1 copy.39
  8.7 1.0 broadcast_in_dim.12
  9.7 4.1 %all-to-all-start = ((bf16[4,256,512]{2,1,0:T(8,128)(2,1)}), bf16[4,256,512]{2,1,0:T(8,128)(2,1)S(1)}, u32[]{:S(2)}, u32[]{:S(2)}) async-start(bf16[4,256,512]{2,1,0:T(8,128)(2,1)} %broadcast_in_dim.12), calls=%async_computation | async-start | bytes 2097152 | tf_op jit(solution)/shard_map/all_to_all | solution.py:22
  13.8 0.0 copy-done.3
  13.8 0.5 copy.40
  14.4 0.1 pad.8
  14.4 13.0 %all-to-all-done = bf16[4,256,512]{2,1,0:T(8,128)(2,1)S(1)} async-done(((bf16[4,256,512]{2,1,0:T(8,128)(2,1)}), bf16[4,256,512]{2,1,0:T(8,128)(2,1)S(1)}, u32[]{:S(2)}, u32[]{:S(2)}) %all-to-all-start) | async-done | bytes 1048608 | tf_op jit(solution)/shard_map/all_to_all | solution.py:22
  27.5 16.1 %all_to_all.50 = bf16[4,256,512]{1,2,0:T(8,128)(2,1)S(1)} all-to-all(bf16[4,256,512]{1,2,0:T(8,128)(2,1)S(1)} %bitcast.34), channel_id=1, replica_groups=mesh['x_lo'=2,'z_hi'=8,'z_lo'=2,'y'=4,'x_hi'=2,'core'=2] {'x_lo','z_lo'}, dimensions={0} | all-to-all | bytes 2097152 | tf_op jit(solution)/shard_map/all_to_all | solution.py:22
  43.5 1.5 broadcast_in_dim.13
  45.0 3.8 %all-to-all-start.1 = ((bf16[2,1024,512]{2,1,0:T(8,128)(2,1)}), bf16[2,1024,512]{2,1,0:T(8,128)(2,1)S(1)}, u32[]{:S(2)}, u32[]{:S(2)}) async-start(bf16[2,1024,512]{2,1,0:T(8,128)(2,1)} %broadcast_in_dim.13), calls=%async_computation.1 | async-start | bytes 4194304 | tf_op jit(solution)/shard_map/all_to_all | solution.py:22
  48.8 0.0 reduce-scatter.2.cloned.1.call-start
  48.8 1.3 copy.41
  50.2 1.5 all-to-all-done.1
  51.6 2.0 convolution_convert_fusion.1
  53.6 0.0 copy-done
  53.6 0.7 convolution_convert_fusion
  54.3 0.0 copy-start.4
  54.3 0.0 copy-start.5
  54.4 1.0 pad_maximum_fusion.1
  55.4 0.0 reduce-scatter.2.cloned.1.call-update
  55.4 57.1 %reduce-scatter.2.cloned.1.call-done = bf16[1,128,512]{2,1,0:T(8,128)(2,1)} async-done(((bf16[8,128,512]{2,1,0:T(8,128)(2,1)}), bf16[1,128,512]{2,1,0:T(8,128)(2,1)}) %reduce-scatter.2.cloned.1.call-update) | async-done | bytes 131088 | tf_op jit(solution)/shard_map/reduce_scatter | solution.py:68
  112.5 8.3 %all_to_all.51 = bf16[4,32,512]{2,1,0:T(8,128)(2,1)S(1)} all-to-all(bf16[4,32,512]{2,1,0:T(8,128)(2,1)} %bitcast.47), channel_id=1, replica_groups=mesh['x_lo'=2,'z_hi'=8,'z_lo'=2,'y'=4,'x_hi'=2,'core'=2] {'x_lo','z_lo'}, dimensions={0} | all-to-all | bytes 262144 | tf_op jit(solution)/shard_map/all_to_all | solution.py:22
  120.8 0.0 copy-done.4
  120.8 0.0 copy-done.5
  120.8 0.8 multiply_reduce_fusion
  121.6 0.6 broadcast_in_dim_broadcast_in_dim.3
  122.2 7.1 %all_to_all.52 = f32[4,8,128]{2,1,0:T(8,128)S(1)} all-to-all(f32[4,8,128]{2,1,0:T(8,128)S(1)} %broadcast_in_dim_broadcast_in_dim.3), channel_id=1, replica_groups=mesh['x_lo'=2,'z_hi'=8,'z_lo'=2,'y'=4,'x_hi'=2,'core'=2] {'x_lo','z_lo'}, dimensions={0} | all-to-all | bytes 32768 | tf_op jit(solution)/shard_map/all_to_all | solution.py:22
  129.3 17.2 %all_to_all.53 = f32[8,8,128]{2,1,0:T(8,128)S(1)} all-to-all(f32[8,8,128]{2,1,0:T(8,128)S(1)} %broadcast_in_dim.14), channel_id=1, replica_groups=mesh['x_lo'=2,'z_hi'=8,'z_lo'=2,'y'=4,'x_hi'=2,'core'=2] {'z_hi'}, dimensions={0} | all-to-all | bytes 65536 | tf_op jit(solution)/shard_map/all_to_all | solution.py:22
  146.5 0.6 broadcast_in_dim.15
  147.1 6.6 %all-to-all-start.6 = ((f32[16,8,128]{2,1,0:T(8,128)}), f32[16,8,128]{2,1,0:T(8,128)S(1)}, u32[]{:S(2)}, u32[]{:S(2)}) async-start(f32[16,8,128]{2,1,0:T(8,128)} %broadcast_in_dim.15), calls=%async_computation.7 | async-start | bytes 131072 | tf_op jit(solution)/shard_map/all_to_all | solution.py:22
  153.8 0.1 fusion.2
  153.9 0.1 reshape.59
  154.0 7.4 %all-to-all-done.6 = f32[16,8,128]{2,1,0:T(8,128)S(1)} async-done(((f32[16,8,128]{2,1,0:T(8,128)}), f32[16,8,128]{2,1,0:T(8,128)S(1)}, u32[]{:S(2)}, u32[]{:S(2)}) %all-to-all-start.6) | async-done | bytes 65568 | tf_op jit(solution)/shard_map/all_to_all | solution.py:22
  161.5 7.4 %all_to_all.54 = bf16[4,32,512]{2,1,0:T(8,128)(2,1)S(1)} all-to-all(bf16[4,32,512]{2,1,0:T(8,128)(2,1)S(1)} %copy.43), channel_id=1, replica_groups=mesh['x_lo'=2,'z_hi'=8,'z_lo'=2,'y'=4,'x_hi'=2,'core'=2] {'x_lo','z_lo'}, dimensions={0} | all-to-all | bytes 262144 | tf_op jit(solution)/shard_map/all_to_all | solution.py:22
  168.9 1.1 stack.3
  169.9 0.0 copy-done.2
  169.9 0.0 copy-done.1
  169.9 6.1 %all-to-all-start.8 = ((bf16[8,128,512]{2,1,0:T(8,128)(2,1)}), bf16[8,128,512]{2,1,0:T(8,128)(2,1)S(1)}, u32[]{:S(2)}, u32[]{:S(2)}) async-start(bf16[8,128,512]{2,1,0:T(8,128)(2,1)} %stack.3), calls=%async_computation.9 | async-start | bytes 2097152 | tf_op jit(solution)/shard_map/all_to_all | solution.py:79
  176.0 0.1 slice_bitcast_fusion.1
  176.1 0.3 pad_maximum_fusion
  176.4 0.5 slice.20
  177.6 51.5 %all-to-all-done.8 = bf16[8,128,512]{2,1,0:T(8,128)(2,1)S(1)} async-done(((bf16[8,128,512]{2,1,0:T(8,128)(2,1)}), bf16[8,128,512]{2,1,0:T(8,128)(2,1)S(1)}, u32[]{:S(2)}, u32[]{:S(2)}) %all-to-all-start.8) | async-done | bytes 1048608 | tf_op jit(solution)/shard_map/all_to_all | solution.py:79
  229.1 1.2 multiply_convert_fusion
  230.4 16.7 %all_to_all.55 = bf16[4,256,512]{2,1,0:T(8,128)(2,1)S(1)} all-to-all(bf16[4,256,512]{2,1,0:T(8,128)(2,1)S(1)} %bitcast.42), channel_id=1, replica_groups=mesh['x_lo'=2,'z_hi'=8,'z_lo'=2,'y'=4,'x_hi'=2,'core'=2] {'x_lo','z_lo'}, dimensions={0} | all-to-all | bytes 2097152 | tf_op jit(solution)/shard_map/all_to_all | solution.py:22
  247.1 0.1 copy.46
  247.3 1.0 slice.25
  (12 shorter events, 0.2 us)
Async XLA Ops:
  8.5 5.3 %copy-start.3 = (bf16[256,1792]{1,0:T(8,128)(2,1)S(1)}, bf16[256,1792]{1,0:T(8,128)(2,1)}, u32[]{:S(2)}) copy-start(bf16[256,1792]{1,0:T(8,128)(2,1)} %param.4) | copy-start | bytes 2752516
  9.7 17.7 %all-to-all-start = ((bf16[4,256,512]{2,1,0:T(8,128)(2,1)}), bf16[4,256,512]{2,1,0:T(8,128)(2,1)S(1)}, u32[]{:S(2)}, u32[]{:S(2)}) async-start(bf16[4,256,512]{2,1,0:T(8,128)(2,1)} %broadcast_in_dim.12), calls=%async_computation | async-start | bytes 2097152 | tf_op jit(solution)/shard_map/all_to_all | solution.py:22
  45.0 6.6 %all-to-all-start.1 = ((bf16[2,1024,512]{2,1,0:T(8,128)(2,1)}), bf16[2,1024,512]{2,1,0:T(8,128)(2,1)S(1)}, u32[]{:S(2)}, u32[]{:S(2)}) async-start(bf16[2,1024,512]{2,1,0:T(8,128)(2,1)} %broadcast_in_dim.13), calls=%async_computation.1 | async-start | bytes 4194304 | tf_op jit(solution)/shard_map/all_to_all | solution.py:22
  48.8 63.7 %reduce-scatter.2.cloned.1.call-start = ((), (), s32[]{:S(2)}) async-start(), calls=%async_computation.11 | async-start | bytes 1179648 | tf_op jit(solution)/shard_map/reduce_scatter | solution.py:68
  50.2 3.4 %copy-start = (bf16[4,256,512]{2,1,0:T(8,128)(2,1)S(1)}, bf16[4,256,512]{2,1,0:T(8,128)(2,1)}, u32[]{:S(2)}) copy-start(bf16[4,256,512]{2,1,0:T(8,128)(2,1)} %copy.41) | copy-start | bytes 3145732
  54.3 66.5 %copy-start.4 = (f32[32,1792]{1,0:T(8,128)S(1)}, f32[32,1792]{1,0:T(8,128)}, u32[]{:S(2)}) copy-start(f32[32,1792]{1,0:T(8,128)} %param.6) | copy-start | bytes 688132
  54.3 66.5 %copy-start.5 = (f32[32,1792]{1,0:T(8,128)S(1)}, f32[32,1792]{1,0:T(8,128)}, u32[]{:S(2)}) copy-start(f32[32,1792]{1,0:T(8,128)} %param.7) | copy-start | bytes 688132
  121.6 48.3 %copy-start.2 = (f32[32,1792]{1,0:T(8,128)}, f32[32,1792]{1,0:T(8,128)S(1)}, u32[]{:S(2)}) copy-start(f32[32,1792]{1,0:T(8,128)S(1)} %get-tuple-element.5) | copy-start | bytes 688132
  121.6 48.3 %copy-start.1 = (f32[32,1792]{1,0:T(8,128)}, f32[32,1792]{1,0:T(8,128)S(1)}, u32[]{:S(2)}) copy-start(f32[32,1792]{1,0:T(8,128)S(1)} %get-tuple-element.4) | copy-start | bytes 688132
  147.1 14.3 %all-to-all-start.6 = ((f32[16,8,128]{2,1,0:T(8,128)}), f32[16,8,128]{2,1,0:T(8,128)S(1)}, u32[]{:S(2)}, u32[]{:S(2)}) async-start(f32[16,8,128]{2,1,0:T(8,128)} %broadcast_in_dim.15), calls=%async_computation.7 | async-start | bytes 131072 | tf_op jit(solution)/shard_map/all_to_all | solution.py:22
  169.9 59.2 %all-to-all-start.8 = ((bf16[8,128,512]{2,1,0:T(8,128)(2,1)}), bf16[8,128,512]{2,1,0:T(8,128)(2,1)S(1)}, u32[]{:S(2)}, u32[]{:S(2)}) async-start(bf16[8,128,512]{2,1,0:T(8,128)(2,1)} %stack.3), calls=%async_computation.9 | async-start | bytes 2097152 | tf_op jit(solution)/shard_map/all_to_all | solution.py:79
Sparse Core Ops, SparseCore 0:
  55.5 56.8 reduce-scatter.1
